TPU v7x, 32 devices: a whole 2x2x4 slice. The times are simulated.
32 devices in a mesh: row: 4 (over z), col: 8 (over y, x, core).
Axes of the slice: x: 2, y: 2, z: 4, core: 2. Of those that a mesh axis runs over, the one named last changes fastest.
Arguments:
- minus_gradient: float32 [6, 16384], P(None, ('row', 'col')), may hold values from -10 to 10
- diag_blocks: float32 [36, 16384], P(None, ('row', 'col')), may hold values from -1000 to 1000, as said below
- hess_blocks: float32 [4, 8, 36, 4096], P('row', 'col'), may hold values from -40 to 40, as said below
- block_rows: int32 [4, 8, 4096], P('row', 'col'), may hold values from 0 to 2047
- block_cols: int32 [4, 8, 4096], P('row', 'col'), may hold values from 0 to 4095
- block_counts: int32 [4, 8], P('row', 'col'), may hold values from 0 to 4096, as said below
Outputs:
- pose_update: float32 [6, 16384], P(None, ('row', 'col'))
- residual: float32 [6, 16384], P(None, ('row', 'col'))
Inputs may be any that keep to these rules, and one draw needn't show every extreme that they name: `hess_blocks`: the live blocks of all tiles together with diag_blocks form a symmetric positive definite matrix; no live block lies on the diagonal; the slots after the live ones hold arbitrary entries. `diag_blocks`: each 6x6 block is symmetric positive definite. The live slots of a tile are its first block_counts slots.
All inputs are finite; a program needn't handle non-finite values.
Results may differ from a plain program's by a relative error of at most 0.0003.
Values sent between devices are 32-bit elements; how exact they have to be, the bound alone decides.
No kernel may reach another device: no remote copies, remote signals or barrier semaphores. Data moves between devices by JAX's collectives and lax.ppermute only.
A program may use at most 64 MiB of HBM per device.

v0:
```python
import math
import jax
import jax.numpy as jnp
from jax import lax
from jax.sharding import PartitionSpec as P

ITERS = 3


def factor_blocks(blocks):
    lower_part = {}
    reciprocals = []
    for j in range(6):
        pivot_value = blocks[7 * j]
        for k in range(j):
            pivot_value = pivot_value - lower_part[j, k] * lower_part[j, k]
        reciprocal = 1.0 / jnp.sqrt(pivot_value)
        reciprocals.append(reciprocal)
        for i in range(j + 1, 6):
            entry_value = blocks[6 * i + j]
            for k in range(j):
                entry_value = entry_value - lower_part[i, k] * lower_part[j, k]
            lower_part[i, j] = entry_value * reciprocal
    return (lower_part, reciprocals)


def apply_inverse(lower_part, reciprocals, vector):
    forward = []
    for i in range(6):
        running = vector[i]
        for k in range(i):
            running = running - lower_part[i, k] * forward[k]
        forward.append(running * reciprocals[i])
    backward = [None] * 6
    for i in range(5, -1, -1):
        running = forward[i]
        for k in range(i + 1, 6):
            running = running - lower_part[k, i] * backward[k]
        backward[i] = running * reciprocals[i]
    return jnp.stack(backward)


def diagonal_term(diag_blocks, vector):
    return jnp.sum(diag_blocks.reshape(6, 6, -1) * vector[None], axis=1)


def pick_columns(source, offsets):
    width = source.shape[1]
    low_width = math.gcd(128, width)
    high_width = width // low_width
    table = source.reshape(6 * high_width, low_width)
    slot_count = offsets.shape[0]
    block_size = math.gcd(512, slot_count)
    turns = slot_count // block_size

    def pick_one_block(carry, offset):
        low_part = offset % low_width
        high_part = offset // low_width
        low_onehot = (
            lax.broadcasted_iota(jnp.int32, (low_width, block_size), 0) == low_part[None, :]
        ).astype(jnp.float32)
        spread = jnp.dot(
            table, low_onehot, precision=lax.Precision.HIGHEST, preferred_element_type=jnp.float32
        )
        high_onehot = (
            lax.broadcasted_iota(jnp.int32, (high_width, block_size), 0) == high_part[None, :]
        ).astype(jnp.float32)
        chosen = jnp.sum(spread.reshape(6, high_width, block_size) * high_onehot[None], axis=1)
        return (carry, chosen)

    unused, blocks_out = lax.scan(pick_one_block, None, offsets.reshape(turns, block_size))
    return jnp.transpose(blocks_out, (1, 0, 2)).reshape(6, slot_count)


def add_rows(terms, rows, span_size):
    low_width = math.gcd(128, span_size)
    high_width = span_size // low_width
    slot_count = rows.shape[0]
    block_size = math.gcd(512, slot_count)
    turns = slot_count // block_size
    term_blocks = jnp.transpose(terms.reshape(6, turns, block_size), (1, 0, 2))
    row_blocks = rows.reshape(turns, block_size)

    def add_one_block(carry, inputs):
        term_block, row_block = inputs
        high_onehot = (
            lax.broadcasted_iota(jnp.int32, (high_width, block_size), 0)
            == (row_block // low_width)[None, :]
        ).astype(jnp.float32)
        spread = (term_block[:, None, :] * high_onehot[None]).reshape(6 * high_width, block_size)
        low_onehot = (
            (row_block % low_width)[:, None]
            == lax.broadcasted_iota(jnp.int32, (block_size, low_width), 1)
        ).astype(jnp.float32)
        carry = carry + jnp.dot(
            spread, low_onehot, precision=lax.Precision.HIGHEST, preferred_element_type=jnp.float32
        )
        return (carry, None)

    start_total = jnp.zeros((6 * high_width, low_width), jnp.float32)
    total, unused = lax.scan(add_one_block, start_total, (term_blocks, row_blocks))
    return total.reshape(6, span_size)


def merged_sums(residual, precond, hess_image):
    return lax.psum((jnp.sum(residual * precond), jnp.sum(hess_image * precond)), ("row", "col"))


def on_device(minus_gradient, diag_blocks, hess_blocks, block_rows, block_cols, block_counts):
    pose_dev = minus_gradient.shape[1]
    blocks = hess_blocks.reshape(6, 6, -1)
    local_rows = block_rows.reshape(-1)
    local_cols = block_cols.reshape(-1)
    slot_count = local_rows.shape[0]
    live_mask = jnp.arange(slot_count, dtype=jnp.int32) < block_counts.reshape(())
    span_size = pose_dev * lax.axis_size("row")
    lower_part, reciprocals = factor_blocks(diag_blocks)

    def tile_terms(picked):
        return jnp.sum(blocks * picked[None], axis=1)

    def hessian(vector):
        gathered = lax.all_gather(vector, "col", axis=1, tiled=True)
        picked = pick_columns(gathered, local_cols)
        live_terms = jnp.where(live_mask[None, :], tile_terms(picked), 0.0)
        partial_value = add_rows(live_terms, local_rows, span_size)
        own_term = diagonal_term(diag_blocks, vector)
        summed = lax.psum(partial_value, "row")
        reduced = lax.dynamic_slice_in_dim(summed, lax.axis_index("row") * pose_dev, pose_dev, 1)
        return reduced + own_term

    solution = jnp.zeros_like(minus_gradient)
    residual = minus_gradient
    precond = apply_inverse(lower_part, reciprocals, residual)
    hess_image = hessian(precond)
    rho_now, curv_value = merged_sums(residual, precond, hess_image)
    step_size = rho_now / curv_value
    direction = precond
    along_image = hess_image
    for k in range(ITERS):
        solution = solution + step_size * direction
        residual = residual - step_size * along_image
        if k + 1 < ITERS:
            precond = apply_inverse(lower_part, reciprocals, residual)
            hess_image = hessian(precond)
            rho_next, curv_value = merged_sums(residual, precond, hess_image)
            ratio_next = rho_next / rho_now
            step_size = rho_next / (curv_value - ratio_next * rho_next / step_size)
            direction = precond + ratio_next * direction
            along_image = hess_image + ratio_next * along_image
            rho_now = rho_next
    return (solution, residual)


def solution(mesh):
    placed = (
        P(None, ("row", "col")),
        P(None, ("row", "col")),
        P("row", "col", None, None),
        P("row", "col", None),
        P("row", "col", None),
        P("row", "col"),
    )
    return jax.shard_map(
        on_device,
        mesh=mesh,
        in_specs=placed,
        out_specs=(P(None, ("row", "col")), P(None, ("row", "col"))),
        check_vma=False,
    )
```

profile of v0, /device:TPU:14, one launch (start us, length us, event | category | flops | bytes accessed | tf_op | source)
XLA Modules:
  0.0 246.8 jit_solution(5160269623161957242)
XLA Ops:
  0.6 1.1 subtract_multiply_fusion.21
  1.7 0.7 copy-done.2
  2.6 8.2 %all_gather.9 = f32[6,4096]{1,0:T(8,128)S(1)} all-gather(f32[6,512]{1,0:T(8,128)S(1)} %stack.6), channel_id=1, replica_groups=mesh['row'=4,'col'=8] {'col'}, dimensions={1}, use_global_device_ids=true | all-gather | bytes 110592 | tf_op jit(solution)/shard_map/all_gather | solution.py:123
  10.9 0.5 broadcast.572
  11.5 0.7 reduce.7
  12.3 3.9 %while.75 = (s32[]{:T(128)}, f32[8,6,512]{2,1,0:T(8,128)S(1)}, s32[8,512]{1,0:T(8,128)S(1)}, f32[192,128]{1,0:T(8,128)S(1)}, s32[]{:T(128)}) while((s32[]{:T(128)}, f32[8,6,512]{2,1,0:T(8,128)S(1)}, s32[8,512]{1,0:T(8,128)S(1)}, f32[192,128]{1,0:T(8,128)S(1)}, s32[]{:T(128)}) %tuple.218), condition=%wide.region_4.5_spmd, body=%wide.region_2.4_spmd.sunk | while | flops 151297024 | bytes 1075269 | solution.py:71
  12.3 0.3 fusion.66
  12.8 0.3 fusion.66
  13.3 0.3 fusion.66
  13.8 0.3 fusion.66
  14.3 0.3 fusion.66
  14.8 0.3 fusion.66
  15.3 0.3 fusion.66
  15.7 0.3 fusion.66
  16.2 1.4 reduce
  18.7 0.7 copy-done.4
  19.4 0.7 reduce.8
  20.1 3.9 %while.78 = (s32[]{:T(128)}, f32[96,128]{1,0:T(8,128)S(1)}, f32[8,6,512]{2,1,0:T(8,128)S(1)}, s32[8,512]{1,0:T(8,128)S(1)}, s32[]{:T(128)}, /*index=5*/s32[]{:T(128)}) while((s32[]{:T(128)}, f32[96,128]{1,0:T(8,128)S(1)}, f32[8,6,512]{2,1,0:T(8,128)S(1)}, s32[8,512]{1,0:T(8,128)S(1)}, s32[]{:T(128)}, /*index=5*/s32[]{:T(128)}) %tuple.221), condition=%wide.region_7.8_spmd.clone, body=%wide.region_6.7_spmd.clone.sunk | while | flops 75666432 | bytes 608343 | solution.py:101
  20.2 0.4 convolution_add_fusion.6
  20.7 0.4 convolution_add_fusion.6
  21.1 0.4 convolution_add_fusion.6
  21.6 0.4 convolution_add_fusion.6
  22.1 0.4 convolution_add_fusion.6
  22.6 0.4 convolution_add_fusion.6
  23.1 0.4 convolution_add_fusion.6
  23.6 0.4 convolution_add_fusion.6
  24.0 16.2 %psum.64 = f32[6,2048]{1,0:T(8,128)S(1)} all-reduce(f32[6,2048]{1,0:T(8,128)S(1)} %reshape.316), channel_id=1, replica_groups=mesh['row'=4,'col'=8] {'row'}, use_global_device_ids=true, to_apply=%region_8.9 | all-reduce | flops 12288 | bytes 98304 | tf_op jit(solution)/shard_map/psum | solution.py:128
  40.3 0.6 multiply_reduce_fusion.13
  40.9 44.0 %all-reduce.2 = (f32[]{:T(128)}, f32[]{:T(128)}) all-reduce(f32[]{:T(128)} %get-tuple-element.394, f32[]{:T(128)} %get-tuple-element.393), channel_id=1, replica_groups=mesh['row'=4,'col'=8] {'row','col'}, use_global_device_ids=true, to_apply=%region_1.2 | all-reduce | flops 2 | bytes 16 | tf_op jit(solution)/shard_map/psum | solution.py:106
  86.4 8.2 %all_gather.10 = f32[6,4096]{1,0:T(8,128)S(1)} all-gather(f32[6,512]{1,0:T(8,128)S(1)} %stack.7), channel_id=1, replica_groups=mesh['row'=4,'col'=8] {'col'}, dimensions={1}, use_global_device_ids=true | all-gather | bytes 110592 | tf_op jit(solution)/shard_map/all_gather | solution.py:123
  94.6 3.9 %while.76 = (s32[]{:T(128)}, f32[8,6,512]{2,1,0:T(8,128)S(1)}, s32[8,512]{1,0:T(8,128)S(1)}, f32[192,128]{1,0:T(8,128)S(1)}, s32[]{:T(128)}) while((s32[]{:T(128)}, f32[8,6,512]{2,1,0:T(8,128)S(1)}, s32[8,512]{1,0:T(8,128)S(1)}, f32[192,128]{1,0:T(8,128)S(1)}, s32[]{:T(128)}) %tuple.236), condition=%wide.region_16.17_spmd, body=%wide.region_14.16_spmd.sunk | while | flops 151297024 | bytes 1075269 | solution.py:71
  94.7 0.3 fusion.69
  95.7 0.3 fusion.69
  97.6 0.3 fusion.69
  98.9 3.9 %while.79 = (s32[]{:T(128)}, f32[96,128]{1,0:T(8,128)S(1)}, f32[8,6,512]{2,1,0:T(8,128)S(1)}, s32[8,512]{1,0:T(8,128)S(1)}, s32[]{:T(128)}, /*index=5*/s32[]{:T(128)}) while((s32[]{:T(128)}, f32[96,128]{1,0:T(8,128)S(1)}, f32[8,6,512]{2,1,0:T(8,128)S(1)}, s32[8,512]{1,0:T(8,128)S(1)}, s32[]{:T(128)}, ...), condition=%wide.region_19.20_spmd.clone, body=%wide.region_18.19_spmd.clone.sunk | while | flops 75666432 | bytes 608343 | solution.py:101
  99.0 0.4 convolution_add_fusion.7
  99.5 0.4 convolution_add_fusion.7
  100.0 0.4 convolution_add_fusion.7
  100.5 0.4 convolution_add_fusion.7
  100.9 0.4 convolution_add_fusion.7
  101.4 0.4 convolution_add_fusion.7
  101.9 0.4 convolution_add_fusion.7
  102.4 0.4 convolution_add_fusion.7
  102.8 14.3 %psum.67 = f32[6,2048]{1,0:T(8,128)S(1)} all-reduce(f32[6,2048]{1,0:T(8,128)S(1)} %reshape.319), channel_id=1, replica_groups=mesh['row'=4,'col'=8] {'row'}, use_global_device_ids=true, to_apply=%region_20.21 | all-reduce | flops 12288 | bytes 98304 | tf_op jit(solution)/shard_map/psum | solution.py:128
  117.1 0.7 multiply_reduce_fusion.11
  117.8 44.2 %all-reduce.1 = (f32[]{:T(128)}, f32[]{:T(128)}) all-reduce(f32[]{:T(128)} %get-tuple-element.392, f32[]{:T(128)} %get-tuple-element.391), channel_id=1, replica_groups=mesh['row'=4,'col'=8] {'row','col'}, use_global_device_ids=true, to_apply=%region_13.14 | all-reduce | flops 2 | bytes 16 | tf_op jit(solution)/shard_map/psum | solution.py:106
  166.7 8.1 %all_gather.11 = f32[6,4096]{1,0:T(8,128)S(1)} all-gather(f32[6,512]{1,0:T(8,128)S(1)} %stack.8), channel_id=1, replica_groups=mesh['row'=4,'col'=8] {'col'}, dimensions={1}, use_global_device_ids=true | all-gather | bytes 110592 | tf_op jit(solution)/shard_map/all_gather | solution.py:123
  174.9 3.9 %while.77 = (s32[]{:T(128)}, f32[8,6,512]{2,1,0:T(8,128)S(1)}, s32[8,512]{1,0:T(8,128)S(1)}, f32[192,128]{1,0:T(8,128)S(1)}, s32[]{:T(128)}) while((s32[]{:T(128)}, f32[8,6,512]{2,1,0:T(8,128)S(1)}, s32[8,512]{1,0:T(8,128)S(1)}, f32[192,128]{1,0:T(8,128)S(1)}, s32[]{:T(128)}) %tuple.237), condition=%wide.region_28.29_spmd, body=%wide.region_26.28_spmd.sunk | while | flops 151297024 | bytes 1075269 | solution.py:71
  175.0 0.3 fusion.72
  175.4 0.3 fusion.72
  177.9 0.3 fusion.72
  179.1 3.9 %while.80 = (s32[]{:T(128)}, f32[96,128]{1,0:T(8,128)S(1)}, f32[8,6,512]{2,1,0:T(8,128)S(1)}, s32[8,512]{1,0:T(8,128)S(1)}, s32[]{:T(128)}, /*index=5*/s32[]{:T(128)}) while((s32[]{:T(128)}, f32[96,128]{1,0:T(8,128)S(1)}, f32[8,6,512]{2,1,0:T(8,128)S(1)}, s32[8,512]{1,0:T(8,128)S(1)}, s32[]{:T(128)}, ...), condition=%wide.region_31.32_spmd.clone, body=%wide.region_30.31_spmd.clone.sunk | while | flops 75666432 | bytes 608343 | solution.py:101
  179.3 0.4 convolution_add_fusion.8
  179.7 0.4 convolution_add_fusion.8
  180.2 0.4 convolution_add_fusion.8
  180.7 0.4 convolution_add_fusion.8
  181.2 0.4 convolution_add_fusion.8
  181.7 0.4 convolution_add_fusion.8
  182.2 0.4 convolution_add_fusion.8
  182.6 0.4 convolution_add_fusion.8
  183.0 14.4 %psum.70 = f32[6,2048]{1,0:T(8,128)S(1)} all-reduce(f32[6,2048]{1,0:T(8,128)S(1)} %reshape.321), channel_id=1, replica_groups=mesh['row'=4,'col'=8] {'row'}, use_global_device_ids=true, to_apply=%region_32.33 | all-reduce | flops 12288 | bytes 98304 | tf_op jit(solution)/shard_map/psum | solution.py:128
  197.5 0.6 multiply_reduce_fusion.9
  198.1 44.1 %all-reduce = (f32[]{:T(128)}, f32[]{:T(128)}) all-reduce(f32[]{:T(128)} %get-tuple-element.390, f32[]{:T(128)} %get-tuple-element.389), channel_id=1, replica_groups=mesh['row'=4,'col'=8] {'row','col'}, use_global_device_ids=true, to_apply=%region_25.26 | all-reduce | flops 2 | bytes 16 | tf_op jit(solution)/shard_map/psum | solution.py:106
  246.2 0.6 multiply_subtract_fusion
  (294 shorter events, 9.0 us)
Async XLA Ops:
  0.6 1.1 copy-start.1
  1.7 0.7 copy-start.2
  10.8 0.7 copy-start.3
  12.2 4.0 %copy-start = (f32[1,1,36,4096]{3,1,2,0:T(1,128)S(1)}, f32[1,1,36,4096]{3,1,2,0:T(1,128)}, u32[]{:S(2)}) copy-start(f32[1,1,36,4096]{3,1,2,0:T(1,128)} %param.20) | copy-start | bytes 1769476
  18.6 0.7 copy-start.4
where the time goes:
time: 248 us; the launch traced here: 247 us
  blocking collectives  202 us (81%)
  matrix products  16.6 us (7%)
  between operations  11.5 us (5%)
  other arithmetic  11.1 us (4%)
  loops' own time  2.93 us (1%)
  local copies, waits for them, and re-layouts  2.92 us (1%)
    psum x3, blocking collectives, merged_sums(): lax.psum((jnp.sum(residual * precond), jnp.sum(hess_image * precond)), ('...  132 us
    psum x3, blocking collectives, hessian(): summed = lax.psum(partial_value, 'row')  44.9 us
    all_gather x3, blocking collectives, hessian(): gathered = lax.all_gather(vector, 'col', axis=1, tiled=True)  24.5 us
    dot_general x24, matrix products, add_one_block(): jnp.dot(spread, low_onehot, precision=lax.Precision.HIGHEST, preferred_el...  8.61 us
    dot_general x24, matrix products, pick_one_block(): jnp.dot(table, low_onehot, precision=lax.Precision.HIGHEST, preferred_ele...  7.99 us

commit v1 on v0

--- a/solution.py
+++ b/solution.py
@@ -125,7 +125,9 @@
         live_terms = jnp.where(live_mask[None, :], tile_terms(picked), 0.0)
         partial_value = add_rows(live_terms, local_rows, span_size)
         own_term = diagonal_term(diag_blocks, vector)
-        summed = lax.psum(partial_value, "row")
+        summed = partial_value
+        for hop in (1, 2):
+            summed = summed + lax.ppermute(summed, "row", [(dev, dev ^ hop) for dev in range(4)])
         reduced = lax.dynamic_slice_in_dim(summed, lax.axis_index("row") * pose_dev, pose_dev, 1)
         return reduced + own_term
 

time: 248 us -> 224 us (0.903)
  blocking collectives: 202 us -> 149 us
  waiting for transfers between devices: 0 us -> 20.6 us
  starting transfers between devices: 0 us -> 8.18 us
    psum x3 -> x0, blocking collectives: 44.9 us -> none  [hessian(): summed = lax.psum(partial_value, 'row')]
    ppermute x0 -> x6, waiting for transfers between devices: none -> 20.6 us  [hessian(): lax.ppermute(summed, 'row', [(dev, dev ^ hop) for dev in range(4)])]
    ppermute x0 -> x6, starting transfers between devices: none -> 8.18 us  [hessian(): lax.ppermute(summed, 'row', [(dev, dev ^ hop) for dev in range(4)])]
    psum x3, blocking collectives: 132 us -> 125 us  [merged_sums(): lax.psum((jnp.sum(residual * precond), jnp.sum(hess_image * precond)), ('...]
  transfers between devices with their start and end apart: 0 -> 6, of which waited for: 0 -> 6; matrix products, arithmetic and copies ran while one was open for 0% -> 0% of each run, Pallas kernels for 0% -> 0%
where the time goes in v1:
time: 224 us; the launch traced here: 223 us
  blocking collectives  149 us (67%)
  waiting for transfers between devices  20.6 us (9%)
  matrix products  16.6 us (7%)
  between operations  11.8 us (5%)
  other arithmetic  11.2 us (5%)
  starting transfers between devices  8.18 us (4%)
  loops' own time  2.91 us (1%)
  local copies, waits for them, and re-layouts  2.25 us (1%)
    psum x3, blocking collectives, merged_sums(): lax.psum((jnp.sum(residual * precond), jnp.sum(hess_image * precond)), ('...  125 us
    all_gather x3, blocking collectives, hessian(): gathered = lax.all_gather(vector, 'col', axis=1, tiled=True)  24.6 us
    ppermute x6, waiting for transfers between devices, hessian(): lax.ppermute(summed, 'row', [(dev, dev ^ hop) for dev in range(4)])  20.6 us
    dot_general x24, matrix products, add_one_block(): jnp.dot(spread, low_onehot, precision=lax.Precision.HIGHEST, preferred_el...  8.61 us
    ppermute x6, starting transfers between devices, hessian(): lax.ppermute(summed, 'row', [(dev, dev ^ hop) for dev in range(4)])  8.18 us
    dot_general x24, matrix products, pick_one_block(): jnp.dot(table, low_onehot, precision=lax.Precision.HIGHEST, preferred_ele...  7.98 us
  transfers between devices with their start and end apart: 6, of which 6 were waited for; matrix products, arithmetic and copies ran while one was open for 0% of the time, Pallas kernels for 0%

profile of v1, /device:TPU:14, one launch (start us, length us, event | category | flops | bytes accessed | tf_op | source)
XLA Modules:
  0.0 223.0 jit_solution(15816408749644590172)
XLA Ops:
  0.7 1.1 subtract_multiply_fusion.21
  1.8 0.7 copy-done.2
  2.6 8.2 %all_gather.9 = f32[6,4096]{1,0:T(8,128)S(1)} all-gather(f32[6,512]{1,0:T(8,128)S(1)} %stack.6), channel_id=1, replica_groups=mesh['row'=4,'col'=8] {'col'}, dimensions={1}, use_global_device_ids=true | all-gather | bytes 110592 | tf_op jit(solution)/shard_map/all_gather | solution.py:123
  10.9 0.6 broadcast.572
  11.5 0.7 reduce.7
  12.3 3.9 %while.75 = (s32[]{:T(128)}, f32[8,6,512]{2,1,0:T(8,128)S(1)}, s32[8,512]{1,0:T(8,128)S(1)}, f32[192,128]{1,0:T(8,128)S(1)}, s32[]{:T(128)}) while((s32[]{:T(128)}, f32[8,6,512]{2,1,0:T(8,128)S(1)}, s32[8,512]{1,0:T(8,128)S(1)}, f32[192,128]{1,0:T(8,128)S(1)}, s32[]{:T(128)}) %tuple.219), condition=%wide.region_4.5_spmd, body=%wide.region_2.4_spmd.sunk | while | flops 151297024 | bytes 1075269 | solution.py:71
  13.3 0.3 fusion.72
  14.8 0.3 fusion.72
  16.2 1.4 reduce
  18.4 0.7 reduce.8
  19.5 3.9 %while.78 = (s32[]{:T(128)}, f32[96,128]{1,0:T(8,128)S(1)}, f32[8,6,512]{2,1,0:T(8,128)S(1)}, s32[8,512]{1,0:T(8,128)S(1)}, s32[]{:T(128)}, /*index=5*/s32[]{:T(128)}) while((s32[]{:T(128)}, f32[96,128]{1,0:T(8,128)S(1)}, f32[8,6,512]{2,1,0:T(8,128)S(1)}, s32[8,512]{1,0:T(8,128)S(1)}, s32[]{:T(128)}, /*index=5*/s32[]{:T(128)}) %tuple.222), condition=%wide.region_7.8_spmd.clone, body=%wide.region_6.7_spmd.clone.sunk | while | flops 75666432 | bytes 608343 | solution.py:101
  19.6 0.4 convolution_add_fusion.6
  20.1 0.4 convolution_add_fusion.6
  20.6 0.4 convolution_add_fusion.6
  21.0 0.4 convolution_add_fusion.6
  21.5 0.4 convolution_add_fusion.6
  22.0 0.4 convolution_add_fusion.6
  22.5 0.4 convolution_add_fusion.6
  23.0 0.4 convolution_add_fusion.6
  23.4 0.5 collective-permute-start
  23.9 3.9 %collective-permute-done = f32[6,2048]{1,0:T(8,128)S(1)} collective-permute-done((f32[6,2048]{1,0:T(8,128)S(1)}, f32[6,2048]{1,0:T(8,128)S(1)}, u32[]{:S(2)}, u32[]{:S(2)}) %collective-permute-start) | collective-permute-done | bytes 49184 | tf_op jit(solution)/shard_map/ppermute | solution.py:130
  27.8 2.7 %collective-permute-start.1 = (f32[6,2048]{1,0:T(8,128)S(1)}, f32[6,2048]{1,0:T(8,128)S(1)}, u32[]{:S(2)}, u32[]{:S(2)}) collective-permute-start(f32[6,2048]{1,0:T(8,128)S(1)} %add.206), channel_id=1, source_target_pairs={{0,16},{8,24},{16,0},{24,8},{1,17},{9,25},{17,1},{25,9},{2,18},{10... | collective-permute-start | bytes 147464 | tf_op jit(solution)/shard_map/ppermute | solution.py:130
  30.5 2.5 %collective-permute-done.1 = f32[6,2048]{1,0:T(8,128)S(1)} collective-permute-done((f32[6,2048]{1,0:T(8,128)S(1)}, f32[6,2048]{1,0:T(8,128)S(1)}, u32[]{:S(2)}, u32[]{:S(2)}) %collective-permute-start.1) | collective-permute-done | bytes 49184 | tf_op jit(solution)/shard_map/ppermute | solution.py:130
  33.0 0.6 multiply_reduce_fusion.13
  33.6 42.2 %all-reduce.2 = (f32[]{:T(128)}, f32[]{:T(128)}) all-reduce(f32[]{:T(128)} %get-tuple-element.394, f32[]{:T(128)} %get-tuple-element.393), channel_id=1, replica_groups=mesh['row'=4,'col'=8] {'row','col'}, use_global_device_ids=true, to_apply=%region_1.2 | all-reduce | flops 2 | bytes 16 | tf_op jit(solution)/shard_map/psum | solution.py:106
  77.4 8.2 %all_gather.10 = f32[6,4096]{1,0:T(8,128)S(1)} all-gather(f32[6,512]{1,0:T(8,128)S(1)} %stack.7), channel_id=1, replica_groups=mesh['row'=4,'col'=8] {'col'}, dimensions={1}, use_global_device_ids=true | all-gather | bytes 110592 | tf_op jit(solution)/shard_map/all_gather | solution.py:123
  85.7 3.9 %while.76 = (s32[]{:T(128)}, f32[8,6,512]{2,1,0:T(8,128)S(1)}, s32[8,512]{1,0:T(8,128)S(1)}, f32[192,128]{1,0:T(8,128)S(1)}, s32[]{:T(128)}) while((s32[]{:T(128)}, f32[8,6,512]{2,1,0:T(8,128)S(1)}, s32[8,512]{1,0:T(8,128)S(1)}, f32[192,128]{1,0:T(8,128)S(1)}, s32[]{:T(128)}) %tuple.239), condition=%wide.region_15.16_spmd, body=%wide.region_13.15_spmd.sunk | while | flops 151297024 | bytes 1075269 | solution.py:71
  87.7 0.3 fusion.75
  89.1 0.3 fusion.75
  89.9 3.9 %while.79 = (s32[]{:T(128)}, f32[96,128]{1,0:T(8,128)S(1)}, f32[8,6,512]{2,1,0:T(8,128)S(1)}, s32[8,512]{1,0:T(8,128)S(1)}, s32[]{:T(128)}, /*index=5*/s32[]{:T(128)}) while((s32[]{:T(128)}, f32[96,128]{1,0:T(8,128)S(1)}, f32[8,6,512]{2,1,0:T(8,128)S(1)}, s32[8,512]{1,0:T(8,128)S(1)}, s32[]{:T(128)}, ...), condition=%wide.region_18.19_spmd.clone, body=%wide.region_17.18_spmd.clone.sunk | while | flops 75666432 | bytes 608343 | solution.py:101
  90.0 0.4 convolution_add_fusion.7
  90.5 0.4 convolution_add_fusion.7
  91.0 0.4 convolution_add_fusion.7
  91.4 0.4 convolution_add_fusion.7
  91.9 0.4 convolution_add_fusion.7
  92.4 0.4 convolution_add_fusion.7
  92.9 0.4 convolution_add_fusion.7
  93.4 0.4 convolution_add_fusion.7
  93.9 4.3 %collective-permute-done.2 = f32[6,2048]{1,0:T(8,128)S(1)} collective-permute-done((f32[6,2048]{1,0:T(8,128)S(1)}, f32[6,2048]{1,0:T(8,128)S(1)}, u32[]{:S(2)}, u32[]{:S(2)}) %collective-permute-start.2) | collective-permute-done | bytes 49184 | tf_op jit(solution)/shard_map/ppermute | solution.py:130
  98.2 1.2 collective-permute-start.3
  99.4 4.0 %collective-permute-done.3 = f32[6,2048]{1,0:T(8,128)S(1)} collective-permute-done((f32[6,2048]{1,0:T(8,128)S(1)}, f32[6,2048]{1,0:T(8,128)S(1)}, u32[]{:S(2)}, u32[]{:S(2)}) %collective-permute-start.3) | collective-permute-done | bytes 49184 | tf_op jit(solution)/shard_map/ppermute | solution.py:130
  103.4 0.7 multiply_reduce_fusion.11
  104.1 40.6 %all-reduce.1 = (f32[]{:T(128)}, f32[]{:T(128)}) all-reduce(f32[]{:T(128)} %get-tuple-element.392, f32[]{:T(128)} %get-tuple-element.391), channel_id=1, replica_groups=mesh['row'=4,'col'=8] {'row','col'}, use_global_device_ids=true, to_apply=%region_12.13 | all-reduce | flops 2 | bytes 16 | tf_op jit(solution)/shard_map/psum | solution.py:106
  149.6 8.2 %all_gather.11 = f32[6,4096]{1,0:T(8,128)S(1)} all-gather(f32[6,512]{1,0:T(8,128)S(1)} %stack.8), channel_id=1, replica_groups=mesh['row'=4,'col'=8] {'col'}, dimensions={1}, use_global_device_ids=true | all-gather | bytes 110592 | tf_op jit(solution)/shard_map/all_gather | solution.py:123
  157.9 3.9 %while.77 = (s32[]{:T(128)}, f32[8,6,512]{2,1,0:T(8,128)S(1)}, s32[8,512]{1,0:T(8,128)S(1)}, f32[192,128]{1,0:T(8,128)S(1)}, s32[]{:T(128)}) while((s32[]{:T(128)}, f32[8,6,512]{2,1,0:T(8,128)S(1)}, s32[8,512]{1,0:T(8,128)S(1)}, f32[192,128]{1,0:T(8,128)S(1)}, s32[]{:T(128)}) %tuple.240), condition=%wide.region_26.27_spmd, body=%wide.region_24.26_spmd.sunk | while | flops 151297024 | bytes 1075269 | solution.py:71
  158.0 0.3 fusion.78
  159.9 0.3 fusion.78
  161.4 0.3 fusion.78
  162.1 3.9 %while.80 = (s32[]{:T(128)}, f32[96,128]{1,0:T(8,128)S(1)}, f32[8,6,512]{2,1,0:T(8,128)S(1)}, s32[8,512]{1,0:T(8,128)S(1)}, s32[]{:T(128)}, /*index=5*/s32[]{:T(128)}) while((s32[]{:T(128)}, f32[96,128]{1,0:T(8,128)S(1)}, f32[8,6,512]{2,1,0:T(8,128)S(1)}, s32[8,512]{1,0:T(8,128)S(1)}, s32[]{:T(128)}, ...), condition=%wide.region_29.30_spmd.clone, body=%wide.region_28.29_spmd.clone.sunk | while | flops 75666432 | bytes 608343 | solution.py:101
  162.2 0.4 convolution_add_fusion.8
  162.7 0.4 convolution_add_fusion.8
  163.2 0.4 convolution_add_fusion.8
  163.7 0.4 convolution_add_fusion.8
  164.2 0.4 convolution_add_fusion.8
  164.7 0.4 convolution_add_fusion.8
  165.2 0.4 convolution_add_fusion.8
  165.6 0.4 convolution_add_fusion.8
  166.0 1.6 collective-permute-start.4
  167.6 2.8 %collective-permute-done.4 = f32[6,2048]{1,0:T(8,128)S(1)} collective-permute-done((f32[6,2048]{1,0:T(8,128)S(1)}, f32[6,2048]{1,0:T(8,128)S(1)}, u32[]{:S(2)}, u32[]{:S(2)}) %collective-permute-start.4) | collective-permute-done | bytes 49184 | tf_op jit(solution)/shard_map/ppermute | solution.py:130
  170.5 2.2 collective-permute-start.5
  172.7 3.0 %collective-permute-done.5 = f32[6,2048]{1,0:T(8,128)S(1)} collective-permute-done((f32[6,2048]{1,0:T(8,128)S(1)}, f32[6,2048]{1,0:T(8,128)S(1)}, u32[]{:S(2)}, u32[]{:S(2)}) %collective-permute-start.5) | collective-permute-done | bytes 49184 | tf_op jit(solution)/shard_map/ppermute | solution.py:130
  175.8 0.6 multiply_reduce_fusion.9
  176.4 42.0 %all-reduce = (f32[]{:T(128)}, f32[]{:T(128)}) all-reduce(f32[]{:T(128)} %get-tuple-element.390, f32[]{:T(128)} %get-tuple-element.389), channel_id=1, replica_groups=mesh['row'=4,'col'=8] {'row','col'}, use_global_device_ids=true, to_apply=%region_23.24 | all-reduce | flops 2 | bytes 16 | tf_op jit(solution)/shard_map/psum | solution.py:106
  222.4 0.6 multiply_subtract_fusion
  (306 shorter events, 11.4 us)
Async XLA Ops:
  0.6 1.1 copy-start.1
  1.7 0.7 copy-start.2
  10.8 0.7 copy-start.3
  12.3 3.9 %copy-start = (f32[1,1,36,4096]{3,1,2,0:T(1,128)S(1)}, f32[1,1,36,4096]{3,1,2,0:T(1,128)}, u32[]{:S(2)}) copy-start(f32[1,1,36,4096]{3,1,2,0:T(1,128)} %param.20) | copy-start | bytes 1769476
  17.7 0.8 copy-start.4
  23.4 4.4 %collective-permute-start = (f32[6,2048]{1,0:T(8,128)S(1)}, f32[6,2048]{1,0:T(8,128)S(1)}, u32[]{:S(2)}, u32[]{:S(2)}) collective-permute-start(f32[6,2048]{1,0:T(8,128)S(1)} %reshape.316), channel_id=1, source_target_pairs={{0,8},{8,0},{16,24},{24,16},{1,9},{9,1},{17,25},{25,17},{2,10},{10... | collective-permute-start | bytes 147464 | tf_op jit(solution)/shard_map/ppermute | solution.py:130
  27.8 5.2 %collective-permute-start.1 = (f32[6,2048]{1,0:T(8,128)S(1)}, f32[6,2048]{1,0:T(8,128)S(1)}, u32[]{:S(2)}, u32[]{:S(2)}) collective-permute-start(f32[6,2048]{1,0:T(8,128)S(1)} %add.206), channel_id=1, source_target_pairs={{0,16},{8,24},{16,0},{24,8},{1,17},{9,25},{17,1},{25,9},{2,18},{10... | collective-permute-start | bytes 147464 | tf_op jit(solution)/shard_map/ppermute | solution.py:130
  93.8 4.4 %collective-permute-start.2 = (f32[6,2048]{1,0:T(8,128)S(1)}, f32[6,2048]{1,0:T(8,128)S(1)}, u32[]{:S(2)}, u32[]{:S(2)}) collective-permute-start(f32[6,2048]{1,0:T(8,128)S(1)} %reshape.319), channel_id=1, source_target_pairs={{0,8},{8,0},{16,24},{24,16},{1,9},{9,1},{17,25},{25,17},{2,10},{10... | collective-permute-start | bytes 147464 | tf_op jit(solution)/shard_map/ppermute | solution.py:130
  98.2 5.2 %collective-permute-start.3 = (f32[6,2048]{1,0:T(8,128)S(1)}, f32[6,2048]{1,0:T(8,128)S(1)}, u32[]{:S(2)}, u32[]{:S(2)}) collective-permute-start(f32[6,2048]{1,0:T(8,128)S(1)} %add.210), channel_id=1, source_target_pairs={{0,16},{8,24},{16,0},{24,8},{1,17},{9,25},{17,1},{25,9},{2,18},{10... | collective-permute-start | bytes 147464 | tf_op jit(solution)/shard_map/ppermute | solution.py:130
  166.0 4.4 %collective-permute-start.4 = (f32[6,2048]{1,0:T(8,128)S(1)}, f32[6,2048]{1,0:T(8,128)S(1)}, u32[]{:S(2)}, u32[]{:S(2)}) collective-permute-start(f32[6,2048]{1,0:T(8,128)S(1)} %reshape.321), channel_id=1, source_target_pairs={{0,8},{8,0},{16,24},{24,16},{1,9},{9,1},{17,25},{25,17},{2,10},{10... | collective-permute-start | bytes 147464 | tf_op jit(solution)/shard_map/ppermute | solution.py:130
  170.5 5.3 %collective-permute-start.5 = (f32[6,2048]{1,0:T(8,128)S(1)}, f32[6,2048]{1,0:T(8,128)S(1)}, u32[]{:S(2)}, u32[]{:S(2)}) collective-permute-start(f32[6,2048]{1,0:T(8,128)S(1)} %add.216), channel_id=1, source_target_pairs={{0,16},{8,24},{16,0},{24,8},{1,17},{9,25},{17,1},{25,9},{2,18},{10... | collective-permute-start | bytes 147464 | tf_op jit(solution)/shard_map/ppermute | solution.py:130
